TPU v7x, 32 devices: a whole 2x2x4 slice. The times are simulated.
32 devices in a mesh: tp: 4 (over z), dp: 8 (over y, x, core).
Axes of the slice: x: 2, y: 2, z: 4, core: 2. Of those that a mesh axis runs over, the one named last changes fastest.
Arguments:
- hidden: bfloat16 [32, 256, 6144], P('dp')
- positions: int32 [256], replicated
- ln1_gain: bfloat16 [6144], replicated
- ln1_bias: bfloat16 [6144], replicated
- w_q: bfloat16 [6144, 6144], P(None, 'tp')
- w_k: bfloat16 [6144, 1024], P(None, 'tp')
- w_v: bfloat16 [6144, 1024], P(None, 'tp')
- w_o: bfloat16 [6144, 6144], P('tp')
- ln2_gain: bfloat16 [6144], replicated
- ln2_bias: bfloat16 [6144], replicated
- w_up: bfloat16 [6144, 24576], P(None, 'tp')
- w_down: bfloat16 [24576, 6144], P('tp')
Outputs:
- output 1: bfloat16 [32, 256, 6144], P('dp')
- output 2: float32 [24576], P('tp')
- output 3: float32 [48], P('tp')
- output 4: float32 [6144], replicated
All inputs are finite; a program needn't handle non-finite values.
Results may differ from a plain program's by a relative error of at most 0.00983148.
Values sent between devices are 32-bit elements.
A program may use at most 1 GiB of HBM per device.

v0:
```python
import jax
import jax.numpy as jnp
from jax import lax
from jax.sharding import PartitionSpec as P

HEAD_DIM = 128
ROT_DIM = 64
ROPE_BASE = 10000.0
LN_EPS = 1e-5


def layer_norm_1p(in_rows, ln_gain, ln_bias):
    rows_f32 = in_rows.astype(jnp.float32)
    row_mean = jnp.mean(rows_f32, axis=-1, keepdims=True)
    centered = rows_f32 - row_mean
    row_var = jnp.mean(centered * centered, axis=-1, keepdims=True)
    scaled = centered * lax.rsqrt(row_var + LN_EPS)
    return (scaled * (1.0 + ln_gain.astype(jnp.float32)) + ln_bias.astype(jnp.float32)).astype(jnp.bfloat16)


def rope_tables(positions):
    rot_half = ROT_DIM // 2
    inv_freq = ROPE_BASE ** (-2.0 * jnp.arange(rot_half, dtype=jnp.float32) / ROT_DIM)
    pos_angle = positions.astype(jnp.float32)[:, None] * inv_freq[None, :]
    return jnp.cos(pos_angle), jnp.sin(pos_angle)


def apply_rope(heads_in, cos_b, sin_b):
    rot_half = ROT_DIM // 2
    heads_f32 = heads_in.astype(jnp.float32)
    lead_half = heads_f32[..., :rot_half]
    tail_half = heads_f32[..., rot_half:ROT_DIM]
    turned = jnp.concatenate([lead_half * cos_b - tail_half * sin_b, tail_half * cos_b + lead_half * sin_b], axis=-1)
    return jnp.concatenate([turned.astype(jnp.bfloat16), heads_in[..., ROT_DIM:]], axis=-1)


def attention_block(h_in, positions, w_q, w_k, w_v):
    n_batch = h_in.shape[0]
    n_seq = h_in.shape[1]
    kv_heads = w_k.shape[1] // HEAD_DIM
    q_group = w_q.shape[1] // w_k.shape[1]
    cos_t, sin_t = rope_tables(positions)
    q_proj = jnp.einsum("bsd,dn->bsn", h_in, w_q, preferred_element_type=jnp.float32).astype(jnp.bfloat16)
    q_proj = q_proj.reshape(n_batch, n_seq, kv_heads, q_group, HEAD_DIM)
    k_proj = jnp.einsum("bsd,dn->bsn", h_in, w_k, preferred_element_type=jnp.float32).astype(jnp.bfloat16)
    k_proj = k_proj.reshape(n_batch, n_seq, kv_heads, HEAD_DIM)
    v_proj = jnp.einsum("bsd,dn->bsn", h_in, w_v, preferred_element_type=jnp.float32).astype(jnp.bfloat16)
    v_proj = v_proj.reshape(n_batch, n_seq, kv_heads, HEAD_DIM)
    q_proj = apply_rope(q_proj, cos_t[None, :, None, None, :], sin_t[None, :, None, None, :])
    k_proj = apply_rope(k_proj, cos_t[None, :, None, :], sin_t[None, :, None, :])
    scores = jnp.einsum("bqkgd,bskd->bkgqs", q_proj, k_proj, preferred_element_type=jnp.float32) * HEAD_DIM ** -0.5
    causal = jnp.arange(n_seq)[:, None] >= jnp.arange(n_seq)[None, :]
    scores = jnp.where(causal, scores, -1e30)
    attn_prob = jax.nn.softmax(scores, axis=-1).astype(jnp.bfloat16)
    return jnp.einsum("bkgqs,bskd->bqkgd", attn_prob, v_proj, preferred_element_type=jnp.float32).astype(jnp.bfloat16)


def solution(mesh):
    def local_layer(hidden, positions, ln1_gain, ln1_bias, w_q, w_k, w_v, w_o, ln2_gain, ln2_bias, w_up, w_down):
        n_batch = hidden.shape[0]
        n_seq = hidden.shape[1]
        h_in = layer_norm_1p(hidden, ln1_gain, ln1_bias)
        attn_out = attention_block(h_in, positions, w_q, w_k, w_v)
        head_norm = jnp.sqrt(jnp.sum(jnp.square(attn_out.astype(jnp.float32)), axis=-1)).reshape(n_batch, n_seq, -1)
        o_part = jnp.einsum("bsn,nd->bsd", attn_out.reshape(n_batch, n_seq, -1), w_o, preferred_element_type=jnp.float32)
        o_sum = lax.psum(o_part, "tp")
        x_mid = (hidden.astype(jnp.float32) + o_sum).astype(jnp.bfloat16)
        h_mid = layer_norm_1p(x_mid, ln2_gain, ln2_bias)
        mlp_act = jnp.square(jax.nn.relu(jnp.einsum("bsd,df->bsf", h_mid, w_up, preferred_element_type=jnp.float32)))
        mlp_part = jnp.einsum("bsf,fd->bsd", mlp_act.astype(jnp.bfloat16), w_down, preferred_element_type=jnp.float32)
        mlp_sum = lax.psum(mlp_part, "tp")
        out_hidden = (x_mid.astype(jnp.float32) + mlp_sum).astype(jnp.bfloat16)
        neuron_sq = jnp.sum(jnp.square(jnp.mean(mlp_act, axis=1)), axis=0)
        head_sq = jnp.sum(jnp.square(jnp.mean(head_norm, axis=1)), axis=0)
        ln1_sq = jnp.sum(jnp.square(jnp.mean(h_in, axis=1, dtype=jnp.float32)), axis=0)
        ln2_sq = jnp.sum(jnp.square(jnp.mean(h_mid, axis=1, dtype=jnp.float32)), axis=0)
        packed = jnp.concatenate([neuron_sq, head_sq, ln1_sq + ln2_sq])
        score_roots = jnp.sqrt(lax.psum(packed, "dp"))
        ff_local = neuron_sq.shape[0]
        heads_local = head_sq.shape[0]
        f_neuron = score_roots[:ff_local]
        f_head = score_roots[ff_local:ff_local + heads_local]
        f_embed = score_roots[ff_local + heads_local:]
        return out_hidden, f_neuron, f_head, f_embed

    weight_col = P(None, "tp")
    weight_row = P("tp", None)
    return jax.shard_map(
        local_layer,
        mesh=mesh,
        in_specs=(P("dp"), P(), P(), P(), weight_col, weight_col, weight_col, weight_row, P(), P(), weight_col, weight_row),
        out_specs=(P("dp"), P("tp"), P("tp"), P()),
        check_vma=False,
    )
```

profile of v0, /device:TPU:0, one launch (start us, length us, event | category | flops | bytes accessed | tf_op | source)
XLA Modules:
  0.0 2060.1 jit_solution(10734685136125649140)
XLA Ops:
  7.3 6.7 convert_reduce_fusion.1
  14.0 8.0 fusion.13
  22.1 10.0 fusion.50
  32.1 1.3 copy.63
  33.4 1.0 slice.38
  34.4 1.1 convert_element_type.79
  35.5 26.6 %fusion.33 = bf16[4,256,1536]{2,1,0:T(8,128)(2,1)S(1)} fusion(bf16[6144,1536]{1,0:T(8,128)(2,1)} %param.16, bf16[4,256,6144]{2,1,0:T(8,128)(2,1)} %param.12, f32[6144]{0:T(1024)S(1)} %convert_element_type.75, f32[6144]{0:T(1024)S(1)} %convert_add_fusion.3, f32[4,256]{1,0:T(4,128)S(1)} %add_rsqrt_fusion.1, f32[4,256]{1,0:T(4,128)S(1)} %broadcast_multiply_fusion.1), kind=kOutput, calls=%fused_computation.46 | convolution fusion | flops 19366674432 | bytes 34660352 | tf_op jit(solution)/shard_map/bsd,dn->bsn/dot_general | solution.py:43
  62.1 2.8 copy.65
  64.9 3.7 copy.66
  68.6 2.6 slice.41
  72.0 9.0 fusion.47
  82.0 2.1 subtract_convert_fusion
  84.2 5.1 fusion.36
  89.3 6.5 fusion.68
  95.8 6.8 multiply_reduce_fusion
  102.6 25.7 %fusion.21 = f32[4,256,6144]{2,1,0:T(8,128)} fusion(bf16[4,256,1536]{1,2,0:T(8,128)(2,1)S(1)} %bitcast.59, bf16[1536,6144]{1,0:T(8,128)(2,1)} %param.19), kind=kOutput, calls=%fused_computation.30 | convolution fusion | flops 19327352832 | bytes 47185920 | tf_op jit(solution)/shard_map/bsn,nd->bsd/dot_general | solution.py:65
  129.0 831.4 %all-reduce.3.cloned.1.call-done = f32[4,256,6144]{2,1,0:T(8,128)} async-done(((f32[4,256,6144]{2,1,0:T(8,128)}), f32[4,256,6144]{2,1,0:T(8,128)}) %all-reduce.3.cloned.1.call-update) | async-done | bytes 25165840 | tf_op jit(solution)/shard_map/psum | solution.py:66
  960.4 20.6 convert_reduce_fusion
  981.0 8.0 fusion.9
  989.0 99.8 %fusion.19 = (f32[4,6144]{1,0:T(4,128)S(1)}, f32[4,256,6144]{2,1,0:T(8,128)}) fusion(bf16[6144,6144]{1,0:T(8,128)(2,1)} %param.22, bf16[4,256,6144]{2,1,0:T(8,128)(2,1)} %get-tuple-element.5, f32[6144]{0:T(1024)S(1)} %convert_element_type.89, f32[6144]{0:T(1024)S(1)} %convert_add_fusion.2, f32[4,256]{1,0:T(4,128)S(1)} %add_rsqrt_fusion, ...), kind=kOutput, calls=%fused_computation.28 | convolution fusion | flops 77366009856 | bytes 113401856 | tf_op jit(solution)/shard_map/bsd,df->bsf/dot_general | solution.py:69
  1088.8 91.4 %fusion.1 = f32[4,256,6144]{2,1,0:T(8,128)} fusion(bf16[6144,6144]{1,0:T(8,128)(2,1)} %param.23, f32[4,256,6144]{2,1,0:T(8,128)} %get-tuple-element.20), kind=kOutput, calls=%fused_computation.1 | convolution fusion | flops 77328285696 | bytes 125829120 | tf_op jit(solution)/shard_map/bsf,fd->bsd/dot_general | solution.py:70
  1181.4 827.1 %all-reduce.5.cloned.1.call-done = f32[4,256,6144]{2,1,0:T(8,128)} async-done(((f32[4,256,6144]{2,1,0:T(8,128)}), f32[4,256,6144]{2,1,0:T(8,128)}) %all-reduce.5.cloned.1.call-update) | async-done | bytes 25165840 | tf_op jit(solution)/shard_map/psum | solution.py:71
  2008.5 19.0 convert_reduce_fusion.2
  2027.8 24.1 %psum.23 = f32[12300]{0:T(1024)S(1)} all-reduce(f32[12300]{0:T(1024)S(1)} %concatenate.17), channel_id=1, replica_groups=mesh['tp'=4,'dp'=8] {'dp'}, use_global_device_ids=true, to_apply=%region_17.18 | all-reduce | flops 12300 | bytes 98400 | tf_op jit(solution)/shard_map/psum | solution.py:78
  (52 shorter events, 5.2 us)
Async XLA Ops:
  7.2 14.9 copy-start
  7.2 953.2 %all-reduce.3.cloned.1.call-start = ((), (), s32[]{:S(2)}) async-start(), calls=%async_computation | async-start | bytes 50331648 | tf_op jit(solution)/shard_map/psum | solution.py:66
  7.3 14.7 copy-start.6
  7.3 14.7 copy-start.7
  64.9 7.1 copy-start.10
  68.6 3.4 copy-start.11
  72.0 9.6 copy-start.2
  81.0 3.2 copy-start.3
  128.3 0.7 copy-start.8
  128.3 0.7 copy-start.9
  128.3 1880.2 %all-reduce.5.cloned.1.call-start = ((), (), s32[]{:S(2)}) async-start(), calls=%async_computation.1 | async-start | bytes 50331648 | tf_op jit(solution)/shard_map/psum | solution.py:71
  1180.2 0.8 copy-start.5
  1181.4 846.2 %copy-start.4 = (f32[4,6144]{1,0:T(4,128)S(1)}, f32[4,6144]{1,0:T(4,128)}, u32[]{:S(2)}) copy-start(f32[4,6144]{1,0:T(4,128)} %get-tuple-element.8) | copy-start | bytes 294916
  2008.5 44.6 %copy-start.1 = (bf16[6144,256]{1,0:T(8,128)(2,1)S(1)}, bf16[6144,256]{1,0:T(8,128)(2,1)}, u32[]{:S(2)}) copy-start(bf16[6144,256]{1,0:T(8,128)(2,1)} %param.17) | copy-start | bytes 9437188
Sparse Core Ops, SparseCore 0:
  128.4 831.9 all-reduce.2
  1180.4 828.0 all-reduce.4
where the time goes:
time: 2070 us; the launch traced here: 2060 us
  waiting for transfers between devices  1660 us (80%)
  matrix products  275 us (13%)
  other arithmetic  74.1 us (4%)
  blocking collectives  24.1 us (1%)
    psum x1, waiting for transfers between devices, local_layer(): o_sum = lax.psum(o_part, 'tp')  831 us
    psum x1, waiting for transfers between devices, local_layer(): mlp_sum = lax.psum(mlp_part, 'tp')  827 us
    dot_general x1, matrix products, local_layer(): jnp.einsum('bsd,df->bsf', h_mid, w_up, preferred_element_type=jnp.float32)  99.8 us
    dot_general x1, matrix products, local_layer(): jnp.einsum('bsf,fd->bsd', mlp_act.astype(jnp.bfloat16), w_down, preferred...  91.4 us
  transfers between devices with their start and end apart: 2, of which 2 were waited for; matrix products, arithmetic and copies ran while one was open for 0% of the time, Pallas kernels for 0%

commit v1 on v0

v1 whole, which is shorter than its diff:
```python
import functools

import jax
import jax.numpy as jnp
from jax import lax
from jax.experimental import pallas as pl
from jax.experimental.pallas import tpu as pltpu
from jax.sharding import PartitionSpec as P

HEAD_DIM = 128
ROT_DIM = 64
ROPE_BASE = 10000.0
LN_EPS = 1e-5
F32 = jnp.float32
BF16 = jnp.bfloat16
MESH_ID = pl.DeviceIdType.MESH

CW = 256
MT = 512
LN_STEPS = 4
WOC = 3
DE = 10
DM = 2
NA = 12
NB = 8
NT = 4
MS_GAP = 24


def rope_tables(positions):
    rot_half = ROT_DIM // 2
    inv_freq = ROPE_BASE ** (-2.0 * jnp.arange(rot_half, dtype=F32) / ROT_DIM)
    pos_angle = positions.astype(F32)[:, None] * inv_freq[None, :]
    cos_t, sin_t = jnp.cos(pos_angle), jnp.sin(pos_angle)
    ones = jnp.ones((positions.shape[0], HEAD_DIM - ROT_DIM), F32)
    cos_full = jnp.concatenate([cos_t, cos_t, ones], axis=1)
    sin_full = jnp.concatenate([-sin_t, sin_t, jnp.zeros_like(ones)], axis=1)
    return cos_full, sin_full


def layer_kernel(dims, x_hbm, cos_ref, sin_ref, g1_ref, b1_ref, g2_ref, b2_ref, wq_hbm, wk_hbm, wv_hbm, wo_hbm, w1_hbm, w2_hbm,
                 y_hbm, p_hbm, on_ref, oh_ref, oe_ref,
                 x_all, h1, h2, act, qk_tmp, k_buf, v_buf, attn, wq_buf, wo_buf, wm_buf,
                 land_a, land_b, pair_sum, total, own_p, stage_o, stage_m,
                 csum1, csum2, nacc, eacc, hacc, stats, stats_in,
                 sem_x, sem_wq, sem_wo, sem_wm, sem_po, sem_pm, sem_own, sem_y,
                 send_a, recv_a, send_b, recv_b, send_st, recv_st):
    n_seq, S, D, FF, QW, KVW, n_dp = dims
    C = D // CW
    K = 2 * n_seq * C
    n_q = QW // KVW
    n_wo = C // WOC
    NPS = LN_STEPS + 2 + n_q + n_wo
    U_Q = LN_STEPS
    U_O = LN_STEPS + 2 + n_q
    G0 = U_O + 1
    n1, n2 = FF // MT, D // MT
    NMS = LN_STEPS + n1 + n2
    MS = C + DE + MS_GAP
    rows = S // LN_STEPS
    group = (QW // HEAD_DIM) // (KVW // HEAD_DIM)
    hpt = KVW // HEAD_DIM
    scale = HEAD_DIM ** -0.5
    LW = D // 8

    z = lax.axis_index("tp")
    me = lax.axis_index("dp")
    is_mid = jnp.logical_or(z == 1, z == 2)
    is_end = jnp.logical_not(is_mid)
    mid_peer = 3 - z
    outer = jnp.where(z == 0, 1, jnp.where(z == 1, 0, jnp.where(z == 2, 3, 2)))

    def x_copy(s):
        return pltpu.make_async_copy(x_hbm.at[s], x_all.at[s], sem_x.at[s])

    def wq_start(i):
        slot = lax.rem(i, 2)

        @pl.when(i == 0)
        def _():
            pltpu.make_async_copy(wk_hbm, wq_buf.at[slot], sem_wq.at[slot]).start()

        @pl.when(i == 1)
        def _():
            pltpu.make_async_copy(wv_hbm, wq_buf.at[slot], sem_wq.at[slot]).start()

        @pl.when(i >= 2)
        def _():
            col = pl.multiple_of((i - 2) * KVW, KVW)
            pltpu.make_async_copy(wq_hbm.at[:, pl.ds(col, KVW)], wq_buf.at[slot], sem_wq.at[slot]).start()

    def wq_wait(i):
        slot = lax.rem(i, 2)
        pltpu.make_async_copy(wk_hbm, wq_buf.at[slot], sem_wq.at[slot]).wait()

    def wo_copy(w):
        slot = lax.rem(w, 2)
        col = pl.multiple_of(w * (WOC * CW), WOC * CW)
        return pltpu.make_async_copy(wo_hbm.at[:, pl.ds(col, WOC * CW)], wo_buf.at[slot], sem_wo.at[slot])

    def wm_start(i):
        slot = lax.rem(i, 2)

        @pl.when(i < n1)
        def _():
            col = pl.multiple_of(i * MT, MT)
            pltpu.make_async_copy(w1_hbm.at[:, pl.ds(col, MT)], wm_buf.at[slot], sem_wm.at[slot]).start()

        @pl.when(i >= n1)
        def _():
            col = pl.multiple_of((i - n1) * MT, MT)
            pltpu.make_async_copy(w2_hbm.at[:, pl.ds(col, MT)], wm_buf.at[slot], sem_wm.at[slot]).start()

    def wm_wait(i):
        slot = lax.rem(i, 2)
        pltpu.make_async_copy(w1_hbm.at[:, pl.ds(0, MT)], wm_buf.at[slot], sem_wm.at[slot]).wait()

    def end_to_mid(k):
        slot = lax.rem(k, NA)
        return pltpu.make_async_remote_copy(
            src_ref=p_hbm.at[k], dst_ref=land_a.at[slot], send_sem=send_a.at[slot], recv_sem=recv_a.at[slot],
            device_id={"tp": outer}, device_id_type=MESH_ID)

    def mid_to_end(k):
        return pltpu.make_async_remote_copy(
            src_ref=total.at[lax.rem(k, NT)], dst_ref=land_a.at[lax.rem(k, NA)], send_sem=send_a.at[lax.rem(k, NT)],
            recv_sem=recv_a.at[lax.rem(k, NA)], device_id={"tp": outer}, device_id_type=MESH_ID)

    def mid_to_mid(k):
        slot = lax.rem(k, NB)
        return pltpu.make_async_remote_copy(
            src_ref=pair_sum.at[slot], dst_ref=land_b.at[slot], send_sem=send_b.at[slot], recv_sem=recv_b.at[slot],
            device_id={"tp": mid_peer}, device_id_type=MESH_ID)

    def own_copy(k):
        slot = lax.rem(k, 2)
        return pltpu.make_async_copy(p_hbm.at[k], own_p.at[slot], sem_own.at[slot])

    def y_copy(k):
        s = lax.rem(lax.div(k, C), n_seq)
        col = pl.multiple_of(lax.rem(k, C) * CW, CW)
        slot = lax.rem(k, 2)
        return pltpu.make_async_copy(x_all.at[s, :, pl.ds(col, CW)], y_hbm.at[s, :, pl.ds(col, CW)], sem_y.at[slot])

    def stats_copy(i):
        peer = lax.rem(me + i, n_dp)
        return pltpu.make_async_remote_copy(
            src_ref=stats, dst_ref=stats_in.at[me], send_sem=send_st.at[i - 1], recv_sem=recv_st.at[me],
            device_id={"dp": peer}, device_id_type=MESH_ID)

    def take_sum(k, value):
        s = lax.rem(lax.div(k, C), n_seq)
        col = pl.multiple_of(lax.rem(k, C) * CW, CW)
        here = x_all.at[s, :, pl.ds(col, CW)]
        here[...] = (here[...].astype(F32) + value).astype(BF16)

    def send_y(k):
        @pl.when(k >= K // 2)
        def _():
            @pl.when(k >= K // 2 + 2)
            def _():
                y_copy(k - 2).wait()
            y_copy(k).start()

    def norm_step(s, step, g_ref, b_ref, dst, csum):
        base = step * rows

        def block(i, carry):
            r0 = pl.multiple_of(base + i * 16, 16)
            v = x_all[s, pl.ds(r0, 16), :].astype(F32)
            mean = jnp.mean(v, axis=-1, keepdims=True)
            cen = v - mean
            var = jnp.mean(cen * cen, axis=-1, keepdims=True)
            out = cen * lax.rsqrt(var + LN_EPS) * (1.0 + g_ref[...].astype(F32)) + b_ref[...].astype(F32)
            dst[pl.ds(r0, 16), :] = out.astype(BF16)
            return carry

        lax.fori_loop(0, rows // 16, block, 0)
        part = jnp.sum(dst[pl.ds(pl.multiple_of(base, rows), rows), :].astype(F32), axis=0, keepdims=True)

        @pl.when(step == 0)
        def _():
            csum[...] = part

        @pl.when(step > 0)
        def _():
            csum[...] += part

        @pl.when(step == LN_STEPS - 1)
        def _():
            mean_c = csum[...] * (1.0 / S)
            eacc[...] += mean_c * mean_c

    lane = lax.broadcasted_iota(jnp.int32, (S, HEAD_DIM), 1)

    def rope(head_bf):
        u = head_bf.astype(F32)
        other = jnp.where(lane < ROT_DIM // 2, pltpu.roll(u, HEAD_DIM - ROT_DIM // 2, 1), pltpu.roll(u, ROT_DIM // 2, 1))
        return (u * cos_ref[...] + other * sin_ref[...]).astype(BF16)

    def attention_step(s, u):
        @pl.when(u == 0)
        def _():
            x_copy(s).wait()

        @pl.when(u < LN_STEPS)
        def _():
            norm_step(s, u, g1_ref, b1_ref, h1, csum1)

        @pl.when(u == LN_STEPS - 2)
        def _():
            @pl.when(s > 0)
            def _():
                wq_start(0)

        @pl.when(jnp.logical_and(u >= U_Q, u < U_O))
        def _():
            i = u - U_Q
            wq_wait(i)

            @pl.when(i + 1 < 2 + n_q)
            def _():
                wq_start(i + 1)

            @pl.when(i == n_q)
            def _():
                wo_copy(0).start()

            r = jnp.dot(h1[...], wq_buf[lax.rem(i, 2)], preferred_element_type=F32)
            qk_tmp[...] = r.astype(BF16)

            @pl.when(i == 0)
            def _():
                for h in range(hpt):
                    k_buf[h] = rope(qk_tmp[:, h * HEAD_DIM:(h + 1) * HEAD_DIM])

            @pl.when(i == 1)
            def _():
                for h in range(hpt):
                    v_buf[h] = qk_tmp[:, h * HEAD_DIM:(h + 1) * HEAD_DIM]

            @pl.when(i >= 2)
            def _():
                qt = i - 2
                kv = lax.div(qt * hpt, group)
                keys = k_buf[kv]
                vals = v_buf[kv]
                row = lax.broadcasted_iota(jnp.int32, (S, S), 0)
                colm = lax.broadcasted_iota(jnp.int32, (S, S), 1)
                causal = row >= colm
                outs = []
                for h in range(hpt):
                    q_h = rope(qk_tmp[:, h * HEAD_DIM:(h + 1) * HEAD_DIM])
                    sc = lax.dot_general(q_h, keys, (((1,), (1,)), ((), ())), preferred_element_type=F32) * scale
                    sc = jnp.where(causal, sc, -1e30)
                    top = jnp.max(sc, axis=-1, keepdims=True)
                    ex = jnp.exp(sc - top)
                    prob = (ex / jnp.sum(ex, axis=-1, keepdims=True)).astype(BF16)
                    outs.append(jnp.dot(prob, vals, preferred_element_type=F32).astype(BF16))
                col = pl.multiple_of(qt * KVW, KVW)
                for h in range(hpt):
                    attn[:, pl.ds(pl.multiple_of(col + h * HEAD_DIM, HEAD_DIM), HEAD_DIM)] = outs[h]
                for h in range(hpt):
                    o_f = attn[:, pl.ds(pl.multiple_of(col + h * HEAD_DIM, HEAD_DIM), HEAD_DIM)].astype(F32)
                    nrm = jnp.sqrt(jnp.sum(o_f * o_f, axis=-1, keepdims=True))
                    mean_n = jnp.sum(nrm, axis=0, keepdims=True) * (1.0 / S)
                    hacc[qt * hpt + h] += jnp.broadcast_to(mean_n * mean_n, (8, HEAD_DIM))

        @pl.when(u >= U_O)
        def _():
            w = u - U_O
            wo_copy(w).wait()

            @pl.when(w + 1 < n_wo)
            def _():
                wo_copy(w + 1).start()

            prod = jnp.dot(attn[...], wo_buf[lax.rem(w, 2)], preferred_element_type=F32)
            for c in range(WOC):
                stage_o[c] = prod[:, c * CW:(c + 1) * CW]
            for c in range(WOC):
                pltpu.make_async_copy(stage_o.at[c], p_hbm.at[C * s + WOC * w + c], sem_po.at[c]).start()

    def attention_step_end(s, u):
        @pl.when(u >= U_O)
        def _():
            for c in range(WOC):
                pltpu.make_async_copy(stage_o.at[c], p_hbm.at[C * s + WOC * (u - U_O) + c], sem_po.at[c]).wait()

    def mlp_step(s, v):
        @pl.when(v < LN_STEPS)
        def _():
            norm_step(s, v, g2_ref, b2_ref, h2, csum2)

        @pl.when(v >= LN_STEPS)
        def _():
            i = v - LN_STEPS
            wm_wait(i)

            @pl.when(i + 1 < n1 + n2)
            def _():
                wm_start(i + 1)

            @pl.when(jnp.logical_and(i + 1 == n1 + n2, s + 1 < n_seq))
            def _():
                wm_start(0)

            @pl.when(i < n1)
            def _():
                up = jnp.dot(h2[...], wm_buf[lax.rem(i, 2)], preferred_element_type=F32)
                up = jnp.maximum(up, 0.0)
                up = up * up
                col = pl.multiple_of(i * MT, MT)
                act[:, pl.ds(col, MT)] = up.astype(BF16)
                mean_n = jnp.sum(up, axis=0, keepdims=True) * (1.0 / S)
                nacc[:, pl.ds(col, MT)] += mean_n * mean_n

            @pl.when(i >= n1)
            def _():
                prod = jnp.dot(act[...], wm_buf[lax.rem(i, 2)], preferred_element_type=F32)
                base = K // 2 + C * s + (MT // CW) * (i - n1)
                for c in range(MT // CW):
                    stage_m[c] = prod[:, c * CW:(c + 1) * CW]
                for c in range(MT // CW):
                    pltpu.make_async_copy(stage_m.at[c], p_hbm.at[base + c], sem_pm.at[c]).start()

    def mlp_step_end(s, v):
        @pl.when(v >= LN_STEPS + n1)
        def _():
            base = K // 2 + C * s + (MT // CW) * (v - LN_STEPS - n1)
            for c in range(MT // CW):
                pltpu.make_async_copy(stage_m.at[c], p_hbm.at[base + c], sem_pm.at[c]).wait()

    def middle_slot(t):
        k = t - DM

        @pl.when(t < K)
        def _():
            @pl.when(t == 0)
            def _():
                own_copy(0).start()

            @pl.when(t + 1 < K)
            def _():
                own_copy(t + 1).start()
            own_copy(t).wait()
            end_to_mid(t).wait_recv()

            @pl.when(t >= NB)
            def _():
                mid_to_mid(t - NB).wait_send()
            pair_sum[lax.rem(t, NB)] = own_p[lax.rem(t, 2)] + land_a[lax.rem(t, NA)]

        @pl.when(jnp.logical_and(k >= 0, k < K))
        def _():
            mid_to_mid(k).wait_recv()

            @pl.when(k >= NT)
            def _():
                mid_to_end(k - NT).wait_send()
            total[lax.rem(k, NT)] = pair_sum[lax.rem(k, NB)] + land_b[lax.rem(k, NB)]

        @pl.when(t < K)
        def _():
            mid_to_mid(t).start()

        @pl.when(jnp.logical_and(k >= 0, k < K))
        def _():
            take_sum(k, total[lax.rem(k, NT)])
            mid_to_end(k).start()
            send_y(k)

    def end_slot(t):
        k = t - DE

        @pl.when(k >= 0)
        def _():
            mid_to_end(k).wait_recv()
            take_sum(k, land_a[lax.rem(k, NA)])
            send_y(k)

        @pl.when(t < K)
        def _():
            @pl.when(t >= NA)
            def _():
                end_to_mid(t - NA).wait_send()
            end_to_mid(t).start()

    x_copy(0).start()
    wq_start(jnp.int32(0))
    for s in range(1, n_seq):
        x_copy(s).start()
    barrier = pltpu.get_barrier_semaphore()
    pl.semaphore_signal(barrier, 1, device_id={"tp": outer}, device_id_type=MESH_ID)

    @pl.when(is_mid)
    def _():
        pl.semaphore_signal(barrier, 1, device_id={"tp": mid_peer}, device_id_type=MESH_ID)
    for i in range(1, n_dp):
        pl.semaphore_signal(barrier, 1, device_id={"dp": lax.rem(me + i, n_dp)}, device_id_type=MESH_ID)

    @pl.when(is_mid)
    def _():
        pl.semaphore_wait(barrier, n_dp + 1)

    @pl.when(is_end)
    def _():
        pl.semaphore_wait(barrier, n_dp)

    nacc[...] = jnp.zeros_like(nacc)
    eacc[...] = jnp.zeros_like(eacc)
    hacc[...] = jnp.zeros_like(hacc)
    stats[...] = jnp.zeros_like(stats)

    def slot(n, carry):
        t = n - G0

        @pl.when(jnp.logical_and(is_mid, t >= 0))
        def _():
            middle_slot(t)

        @pl.when(jnp.logical_and(is_end, t >= 0))
        def _():
            end_slot(t)

        s_a = lax.div(n, NPS)
        u_a = lax.rem(n, NPS)

        @pl.when(n < n_seq * NPS)
        def _():
            attention_step(s_a, u_a)

        @pl.when(t == MS - 2)
        def _():
            wm_start(jnp.int32(0))

        m = jnp.maximum(t - MS, 0)
        s_m = lax.div(m, NMS)
        v_m = lax.rem(m, NMS)
        in_mlp = jnp.logical_and(t >= MS, t < MS + n_seq * NMS)

        @pl.when(in_mlp)
        def _():
            mlp_step(s_m, v_m)

        @pl.when(n < n_seq * NPS)
        def _():
            attention_step_end(s_a, u_a)

        @pl.when(in_mlp)
        def _():
            mlp_step_end(s_m, v_m)

        @pl.when(t == MS + n_seq * NMS)
        def _():
            for r in range(FF // LW):
                stats[r:r + 1, :] = nacc[:, r * LW:(r + 1) * LW]
            for r in range(8):
                stats[8 + r:9 + r, :] = eacc[:, r * LW:(r + 1) * LW]
            per_row = LW // HEAD_DIM
            for h in range(QW // HEAD_DIM):
                stats[16 + h // per_row:17 + h // per_row, (h % per_row) * HEAD_DIM:(h % per_row + 1) * HEAD_DIM] = hacc[h, 0:1, :]

        @pl.when(t == MS + n_seq * NMS + 1)
        def _():
            for i in range(1, n_dp):
                stats_copy(i).start()
        return carry

    lax.fori_loop(0, G0 + K + DE, slot, 0)

    @pl.when(is_mid)
    def _():
        for i in range(NB):
            mid_to_mid(K - NB + i).wait_send()
        for i in range(NT):
            mid_to_end(K - NT + i).wait_send()

    @pl.when(is_end)
    def _():
        for i in range(NA):
            end_to_mid(K - NA + i).wait_send()

    stats_in[me] = stats[...]
    for i in range(1, n_dp):
        peer = lax.rem(me + i, n_dp)
        pltpu.make_async_remote_copy(
            src_ref=stats, dst_ref=stats_in.at[peer], send_sem=send_st.at[i - 1], recv_sem=recv_st.at[peer],
            device_id={"dp": peer}, device_id_type=MESH_ID).wait_recv()
        stats_copy(i).wait_send()
    acc = stats_in[0]
    for i in range(1, n_dp):
        acc = acc + stats_in[i]
    stats[...] = jnp.sqrt(acc)
    for r in range(FF // LW):
        on_ref[:, r * LW:(r + 1) * LW] = stats[r:r + 1, :]
    for r in range(8):
        oe_ref[:, r * LW:(r + 1) * LW] = stats[8 + r:9 + r, :]
    per_row = LW // HEAD_DIM
    for h in range(QW // HEAD_DIM):
        oh_ref[h:h + 1, :] = stats[16 + h // per_row:17 + h // per_row, (h % per_row) * HEAD_DIM:(h % per_row + 1) * HEAD_DIM]
    for i in range(2):
        y_copy(K - 2 + i).wait()


def run_layer(n_dp, hidden, cos_t, sin_t, g1, b1, g2, b2, w_q, w_k, w_v, w_o, w_up, w_down):
    n_seq, S, D = hidden.shape
    QW, KVW, FF = w_q.shape[1], w_k.shape[1], w_up.shape[1]
    C = D // CW
    K = 2 * n_seq * C
    n_q = QW // KVW
    n_heads = QW // HEAD_DIM
    LW = D // 8
    NPS = LN_STEPS + 2 + n_q + C // WOC
    MS = C + DE + MS_GAP
    NMS = LN_STEPS + FF // MT + D // MT
    for s in range(n_seq):
        for j in range(C):
            if s or j >= WOC:
                assert NPS * s + j // WOC - 1 <= C * s + j - 2, "late projection"
            assert MS + NMS * s + LN_STEPS + FF // MT + j // (MT // CW) <= K // 2 + C * s + j - 2, "late product"
        assert MS + NMS * s >= C * (s + 1) + DE, "early MLP"
    assert MS + n_seq * NMS + 2 < K + DE, "late scores"
    assert (QW // KVW) % 1 == 0 and FF == D and C % WOC == 0
    any_spec = pl.BlockSpec(memory_space=pl.ANY)
    vmem_spec = pl.BlockSpec(memory_space=pltpu.VMEM)
    dma = pltpu.SemaphoreType.DMA
    macs = n_seq * S * (D * (QW + 2 * KVW) + QW * D + 2 * D * FF)
    return pl.pallas_call(
        functools.partial(layer_kernel, (n_seq, S, D, FF, QW, KVW, n_dp)),
        out_shape=(
            jax.ShapeDtypeStruct((n_seq, S, D), BF16),
            jax.ShapeDtypeStruct((K, S, CW), F32),
            jax.ShapeDtypeStruct((1, FF), F32),
            jax.ShapeDtypeStruct((n_heads, HEAD_DIM), F32),
            jax.ShapeDtypeStruct((1, D), F32),
        ),
        in_specs=[any_spec] + [vmem_spec] * 6 + [any_spec] * 6,
        out_specs=(any_spec, any_spec, vmem_spec, vmem_spec, vmem_spec),
        scratch_shapes=[
            pltpu.VMEM((n_seq, S, D), BF16),
            pltpu.VMEM((S, D), BF16),
            pltpu.VMEM((S, D), BF16),
            pltpu.VMEM((S, FF), BF16),
            pltpu.VMEM((S, KVW), BF16),
            pltpu.VMEM((KVW // HEAD_DIM, S, HEAD_DIM), BF16),
            pltpu.VMEM((KVW // HEAD_DIM, S, HEAD_DIM), BF16),
            pltpu.VMEM((S, QW), BF16),
            pltpu.VMEM((2, D, KVW), BF16),
            pltpu.VMEM((2, QW, WOC * CW), BF16),
            pltpu.VMEM((2, D, MT), BF16),
            pltpu.VMEM((NA, S, CW), F32),
            pltpu.VMEM((NB, S, CW), F32),
            pltpu.VMEM((NB, S, CW), F32),
            pltpu.VMEM((NT, S, CW), F32),
            pltpu.VMEM((2, S, CW), F32),
            pltpu.VMEM((WOC, S, CW), F32),
            pltpu.VMEM((MT // CW, S, CW), F32),
            pltpu.VMEM((1, D), F32),
            pltpu.VMEM((1, D), F32),
            pltpu.VMEM((1, FF), F32),
            pltpu.VMEM((1, D), F32),
            pltpu.VMEM((n_heads, 8, HEAD_DIM), F32),
            pltpu.VMEM((24, LW), F32),
            pltpu.VMEM((n_dp, 24, LW), F32),
            dma((n_seq,)), dma((2,)), dma((2,)), dma((2,)), dma((WOC,)), dma((MT // CW,)), dma((2,)), dma((2,)),
            dma((NA,)), dma((NA,)), dma((NB,)), dma((NB,)), dma((n_dp - 1,)), dma((n_dp,)),
        ],
        compiler_params=pltpu.CompilerParams(collective_id=0, has_side_effects=True, vmem_limit_bytes=67043328),
        cost_estimate=pl.CostEstimate(flops=2 * macs, bytes_accessed=2 * macs // S, transcendentals=0),
        name="layer",
    )(hidden, cos_t, sin_t, g1, b1, g2, b2, w_q, w_k, w_v, w_o, w_up, w_down)


def solution(mesh):
    n_dp = mesh.shape["dp"]

    def local_layer(hidden, positions, ln1_gain, ln1_bias, w_q, w_k, w_v, w_o, ln2_gain, ln2_bias, w_up, w_down):
        cos_t, sin_t = rope_tables(positions)
        y, _, f_n, f_h, f_e = run_layer(
            n_dp, hidden, cos_t, sin_t, ln1_gain[None], ln1_bias[None], ln2_gain[None], ln2_bias[None],
            w_q, w_k, w_v, w_o, w_up, w_down)
        return y, f_n[0], f_h[:, 0], f_e[0]

    weight_col = P(None, "tp")
    weight_row = P("tp", None)
    return jax.shard_map(
        local_layer,
        mesh=mesh,
        in_specs=(P("dp"), P(), P(), P(), weight_col, weight_col, weight_col, weight_row, P(), P(), weight_col, weight_row),
        out_specs=(P("dp"), P("tp"), P("tp"), P()),
        check_vma=False,
    )
```

time: 2070 us -> 1150 us (0.56)
  waiting for transfers between devices: 1660 us -> 0 us
  Pallas kernels: 0 us -> 1130 us
  matrix products: 275 us -> 0 us
  other arithmetic: 74.1 us -> 2.06 us
  blocking collectives: 24.1 us -> 0 us
    psum x2 -> x0, waiting for transfers between devices: 1660 us -> none  [the longest x1 831 us: local_layer(): o_sum = lax.psum(o_part, 'tp')]
    pallas_call x0 -> x1, Pallas kernels: none -> 1130 us  [run_layer(): pl.pallas_call(functools.partial(layer_kernel, (n_seq, S, D, FF, QW, KVW,...]
    dot_general x8 -> x0, matrix products: 275 us -> none  [the longest x1 99.8 us: local_layer(): jnp.einsum('bsd,df->bsf', h_mid, w_up, preferred_element_type=jnp.float32)]
    reduce_sum x9 -> x0, other arithmetic: 62.6 us -> none  [the longest x2 27.3 us: layer_norm_1p(): row_mean = jnp.mean(rows_f32, axis=-1, keepdims=True)]
    psum x1 -> x0, blocking collectives: 24.1 us -> none  [local_layer(): score_roots = jnp.sqrt(lax.psum(packed, 'dp'))]
  transfers between devices with their start and end apart: 2 -> 0, of which waited for: 2 -> 0; matrix products, arithmetic and copies ran while one was open for 0% -> 0% of each run, Pallas kernels for 0% -> 0%
where the time goes in v1:
time: 1150 us
  Pallas kernels  1130 us (98%)
  local copies, waits for them, and re-layouts  18.8 us (2%)
    pallas_call x1, Pallas kernels, run_layer(): pl.pallas_call(functools.partial(layer_kernel, (n_seq, S, D, FF, QW, KVW,...  1130 us

profile of v1, /device:TPU:0, one launch (start us, length us, event | category | flops | bytes accessed | tf_op | source)
XLA Modules:
  0.0 1152.8 jit_solution(327399611507508085)
XLA Ops:
  0.6 0.1 pad.5.clone
  0.7 0.1 pad.2.clone
  0.8 0.7 convert_element_type.3
  1.5 1.3 broadcast_in_dim.22.g1_ref
  2.8 1.3 broadcast_in_dim.23.b1_ref
  4.1 1.3 broadcast_in_dim.24.g2_ref
  5.5 1.3 broadcast_in_dim.25.b2_ref
  6.8 0.5 fusion
  7.3 0.8 maximum_maximum_fusion
  8.2 1131.3 %layer.1 = (bf16[4,256,6144]{2,1,0:T(8,128)(2,1)}, f32[192,256,256]{2,1,0:T(8,128)}, f32[1,6144]{1,0:T(1,128)}, f32[12,128]{1,0:T(8,128)}, f32[1,6144]{1,0:T(1,128)}) custom-call(bf16[4,256,6144]{2,1,0:T(8,128)(2,1)} %x_hbm.1, f32[256,128]{1,0:T(8,128)} %get-tuple-element.15.cos_ref, f32[256,128]{1,0:T(8,128)} %get-tuple-element.16.sin_ref, ...), custom_call_target="tpu_custom_call" | custom-call | flops 199715979264 | bytes 780140544 | tf_op jit(solution)/shard_map/layer/pallas_call | solution.py:529
  1139.5 0.0 copy-start.1
  1139.5 0.0 copy-start
  1139.5 1.3 slice_reduce_fusion
  1140.8 10.7 copy.20
  1151.5 0.0 copy-done.1
  1151.5 0.6 copy.21
  1152.1 0.0 copy-done
  1152.1 0.6 copy.22
  (3 shorter events, 0.0 us)
Async XLA Ops:
  1139.5 12.1 %copy-start.1 = (f32[1,6144]{1,0:T(1,128)S(1)}, f32[1,6144]{1,0:T(1,128)}, u32[]{:S(2)}) copy-start(f32[1,6144]{1,0:T(1,128)} %get-tuple-element.9) | copy-start | bytes 73732
  1139.5 12.7 %copy-start = (f32[1,6144]{1,0:T(1,128)S(1)}, f32[1,6144]{1,0:T(1,128)}, u32[]{:S(2)}) copy-start(f32[1,6144]{1,0:T(1,128)} %get-tuple-element.11) | copy-start | bytes 73732
